TPU v7x, 8 devices: a whole 2x2x1 slice. The times are simulated.
8 devices in a mesh: dp: 2 (over z, y), tp: 4 (over x, core).
Axes of the slice: x: 2, y: 2, z: 1, core: 2. Of those that a mesh axis runs over, the one named last changes fastest.
Arguments:
- hidden: bfloat16 [4, 256, 7168], P('dp', 'tp'), parts along dimension 0
- lengths: int32 [4], P('dp'), parts along dimension 0
- rope_cos: float32 [4, 256, 32], P('dp'), parts along dimension 0
- rope_sin: float32 [4, 256, 32], P('dp'), parts along dimension 0
- cache_lat: bfloat16 [4, 2304, 512], P('dp'), parts along dimension 0
- cache_pe: bfloat16 [4, 2304, 64], P('dp'), parts along dimension 0
- norm_in: float32 [7168], replicated
- w_dq: bfloat16 [7168, 1536], replicated
- norm_q: float32 [1536], replicated
- w_dkv: bfloat16 [7168, 576], replicated
- norm_kv: float32 [512], replicated
- w_uq: bfloat16 [1536, 64, 192], P(None, 'tp')
- w_uk: bfloat16 [512, 64, 128], P(None, 'tp')
- w_uv: bfloat16 [512, 64, 128], P(None, 'tp')
- w_out: bfloat16 [8192, 7168], P('tp')
Outputs:
- output 1: bfloat16 [4, 256, 7168], P('dp', 'tp'), parts along dimension 0
- output 2: bfloat16 [4, 2304, 512], P('dp'), parts along dimension 0
- output 3: bfloat16 [4, 2304, 64], P('dp'), parts along dimension 0
There are 2 independent parts. A program takes and returns all parts, laid end to end along the dimension named above; an argument that names none is the same for every part.
All inputs are finite; a program needn't handle non-finite values.
Results may differ from a plain program's by a relative error of at most 0.0160033.
Values are sent between devices in bfloat16 or wider.
A program may use at most 1 GiB of HBM per device.

v0:
```python
import functools

import jax
import jax.numpy as jnp
from jax import lax
from jax.experimental import pallas as pl
from jax.experimental.pallas import tpu as pltpu
from jax.sharding import PartitionSpec as P

F32 = jnp.float32
BF16 = jnp.bfloat16
EPS = 1e-6
MIB = 1 << 20
VMEM_ALL = 67043328
MESH = pl.DeviceIdType.MESH
LAT_W = 2176
PREFIX = 2048
ROW_BLK = 512
CHUNK = 512
DEPTH = 512
CHUNKS = 7168 // CHUNK
C2 = 192.0 ** -0.5 * 1.4426950408889634
NEG = -1e30
LOC = 64
HD = 128
NEW = 256
QR = 1536
WID = 2048
CB = 768
KVR = 512
NT = (((1,), (1,)), ((), ()))


def dot(lhs, rhs):
    return jnp.dot(lhs, rhs, preferred_element_type=F32)


def dot_nt(lhs, rhs):
    return lax.dot_general(lhs, rhs, NT, preferred_element_type=F32)


def cost(flops, nbytes):
    return pl.CostEstimate(flops=int(flops), bytes_accessed=int(nbytes), transcendentals=0)


def cache_kernel(len_ref, c_hbm, pe_hbm, cn_hbm, kn_hbm, co_hbm, po_hbm, rows, cols, cn, kn, in_sem, out_sem, side_sem):
    blocks = rows.shape[1] // NEW
    span = lambda r: pl.ds(r * NEW, NEW)
    lat_in = lambda b, r: pltpu.make_async_copy(c_hbm.at[b, span(r)], rows.at[b, span(r)], in_sem.at[b, r])
    lat_out = lambda b, r: pltpu.make_async_copy(rows.at[b, span(r)], co_hbm.at[b, span(r)], out_sem.at[b, r])
    pe_in = lambda b: pltpu.make_async_copy(pe_hbm.at[b], cols.at[b], in_sem.at[b, blocks])
    pe_out = lambda b: pltpu.make_async_copy(cols.at[b], po_hbm.at[b], out_sem.at[b, blocks])
    new_in = [pltpu.make_async_copy(cn_hbm, cn, side_sem.at[0]), pltpu.make_async_copy(kn_hbm, kn, side_sem.at[1])]
    places = [(b, r) for b in range(2) for r in range(blocks)]
    for copy in new_in:
        copy.start()
    for b, r in places:
        lat_in(b, r).start()
    for b in range(2):
        pe_in(b).start()
    for copy in new_in:
        copy.wait()
    for b, r in places:
        shift = r * NEW - len_ref[b]
        lat_in(b, r).wait()

        @pl.when((shift < NEW) & (shift > -NEW))
        def _():
            row = lax.broadcasted_iota(jnp.int32, (NEW, NEW), 0) + shift
            hot = (row == lax.broadcasted_iota(jnp.int32, (NEW, NEW), 1)).astype(F32).astype(BF16)
            row = lax.broadcasted_iota(jnp.int32, (NEW, KVR), 0) + shift
            old = rows[b, span(r), :].astype(F32)
            rows[b, span(r), :] = jnp.where((row >= 0) & (row < NEW), dot(hot, cn[b]), old).astype(BF16)

        lat_out(b, r).start()
    for b in range(2):
        pe_in(b).wait()
        for r in range(blocks):
            shift = r * NEW - len_ref[b]

            @pl.when((shift < NEW) & (shift > -NEW))
            def _():
                row = lax.broadcasted_iota(jnp.int32, (NEW, NEW), 0) + shift
                hot = (row == lax.broadcasted_iota(jnp.int32, (NEW, NEW), 1)).astype(F32).astype(BF16)
                col = lax.broadcasted_iota(jnp.int32, (LOC, NEW), 1) + shift
                old = cols[b, :, span(r)].astype(F32)
                cols[b, :, span(r)] = jnp.where((col >= 0) & (col < NEW), dot_nt(kn[b], hot), old).astype(BF16)

        pe_out(b).start()
    for b, r in places:
        lat_out(b, r).wait()
    for b in range(2):
        pe_out(b).wait()


def update_caches(lengths, cache_lat, pe_t, c_new, k_newt):
    hbm = pl.BlockSpec(memory_space=pl.ANY)
    sems = pltpu.SemaphoreType.DMA((2, cache_lat.shape[1] // NEW + 1))
    return pl.pallas_call(
        cache_kernel,
        in_specs=[pl.BlockSpec(memory_space=pltpu.SMEM)] + [hbm] * 4,
        out_specs=[hbm] * 2,
        out_shape=[jax.ShapeDtypeStruct(v.shape, BF16) for v in (cache_lat, pe_t)],
        scratch_shapes=[*[pltpu.VMEM(v.shape, BF16) for v in (cache_lat, pe_t, c_new, k_newt)], sems, sems, pltpu.SemaphoreType.DMA((2,))],
        compiler_params=pltpu.CompilerParams(vmem_limit_bytes=VMEM_ALL),
        cost_estimate=cost(4e9, 12 * MIB),
        name="caches",
    )(lengths, cache_lat, pe_t, c_new, k_newt)


def at(start, size):
    return pl.ds(pl.multiple_of(start, size), size)


def main_kernel(len_ref, cos, sin, pet, g1, gq, gkv, x_hbm, wdq_hbm, wdkvt_hbm, c_hbm, wuk_hbm, wuv_hbm, wq_hbm, wo_hbm,
                y_hbm, cnew_hbm, knewt_hbm,
                lat, qa, kva, latb, cqt, cn, kn, knt, pe, mask, cbuf, kb, vtb, wkb, wvtb, wqb, q_lo, q_hi, sb, mb, ob, lhsb, wob,
                stage_d, xbuf, stage_x, rbuf, ownb, ybuf,
                lat_send, lat_recv, dq_sem, dkv_sem, c_sem, wk_sem, wvt_sem, wq_sem, wo_sem, x_sem, out_sem, y_sem,
                d_send, d_recv, i_send, i_recv, free_sem):
    me = lax.axis_index("tp")
    chip = me // 2
    core = me % 2
    sib = 2 * chip + (1 - core)
    far = 2 * (1 - chip) + core
    diag = 2 * (1 - chip) + (1 - core)

    def remote(src, dst, send, recv, peer):
        return pltpu.make_async_remote_copy(src_ref=src, dst_ref=dst, send_sem=send, recv_sem=recv, device_id={"tp": peer}, device_id_type=MESH)

    def fetch_rows(src, dst, sem, parts):
        size = dst.shape[0] // parts
        for k in range(parts):
            rows = pl.ds(k * size, size)
            pltpu.make_async_copy(src.at[rows], dst.at[rows], sem).start()

    def c_refs(b):
        return c_hbm.at[b, pl.ds(0, PREFIX), :], cbuf, c_sem

    def wq_refs(h):
        return wq_hbm.at[pl.ds(2 * h, 2)], wqb.at[h % 3], wq_sem.at[h % 3]

    def fetch_wq(i):
        src, dst, sem = wq_refs(i)
        for k in range(2):
            fetch_rows(src.at[k], dst.at[k], sem, 2)

    def wo_refs(g, n):
        return wo_hbm.at[:, at(n * CHUNK, CHUNK)], wob.at[g % 3], wo_sem.at[g % 3]

    def dq_refs(n):
        return wdq_hbm.at[at(n * DEPTH, DEPTH), :], kb.at[at((n % 4) * DEPTH, DEPTH), pl.ds(0, QR)], dq_sem.at[n % 4]

    def dkv_refs(n):
        return wdkvt_hbm.at[:, at(n * DEPTH, DEPTH)], vtb.at[pl.ds(0, 576), at((n % 4) * DEPTH, DEPTH)], dkv_sem.at[n % 4]

    def uk_copy(j):
        return pltpu.make_async_copy(wuk_hbm.at[pl.ds(WID * j, WID), :], kb.at[pl.ds(0, WID), pl.ds(QR + HD * j, HD)], wk_sem.at[j])

    def uv_copy(j):
        return pltpu.make_async_copy(wuv_hbm.at[pl.ds(1024 * j, 1024), :], vtb.at[pl.ds(1024, 1024), pl.ds(HD * j, HD)], wvt_sem.at[j])

    def piece(j):
        return at(HD * (j + 8), HD), pl.ds(1024, 1024)

    def x_copy(j):
        return pltpu.make_async_copy(x_hbm.at[:, at(1024 * j, 1024)], vtb.at[piece(j)], x_sem.at[j])

    def x_again(j):
        return pltpu.make_async_copy(x_hbm.at[:, at(1024 * j, 1024)], kb.at[at(HD * j, HD), pl.ds(0, 1024)], x_sem.at[j])

    for j in range(7):
        x_copy(j).start()
    for n in range(3):
        fetch_rows(*dq_refs(n), 2)
        fetch_rows(*dkv_refs(n), 2)

    barrier = pltpu.get_barrier_semaphore()
    for peer in (sib, far):
        pl.semaphore_signal(barrier, inc=1, device_id={"tp": peer}, device_id_type=MESH)

    aug = jnp.where(lax.broadcasted_iota(jnp.int32, (LOC, NEW), 0) == 0, 1.0, 0.0).astype(BF16)
    causal = lax.broadcasted_iota(jnp.int32, (NEW, NEW), 0) <= lax.broadcasted_iota(jnp.int32, (NEW, NEW), 1)
    for b in range(2):
        sb[pl.ds(NEW * b, NEW), :32] = cos[b].T
        sb[pl.ds(KVR + NEW * b, NEW), :32] = sin[b].T
    qa[...] = jnp.zeros_like(qa)
    kva[...] = jnp.zeros_like(kva)
    for j in range(7):
        x_copy(j).wait()

    def squares(j, acc):
        v = vtb[piece(j)].astype(F32)
        v = v * v
        return acc + sum(v[:, HD * k:HD * k + HD] for k in range(8))

    total = lax.fori_loop(0, 7, squares, jnp.zeros((HD, HD), F32))
    inv_x = lax.rsqrt(jnp.sum(total, axis=-1, keepdims=True) / 7168.0 + EPS)

    def scaled(j, carry):
        vtb[piece(j)] = (vtb[piece(j)].astype(F32) * inv_x * g1[:, at(1024 * j, 1024)]).astype(BF16)
        return carry

    lax.fori_loop(0, 7, scaled, 0)

    def project(n, carry):
        @pl.when(n + 3 < CHUNKS)
        def _():
            fetch_rows(*dq_refs(n + 3), 2)
            fetch_rows(*dkv_refs(n + 3), 2)

        pltpu.make_async_copy(*dq_refs(n)).wait()
        pltpu.make_async_copy(*dkv_refs(n)).wait()

        @pl.when(n == 7)
        def _():
            for j in range(4):
                uk_copy(j).start()
            for j in range(8):
                uv_copy(j).start()

        a = vtb[at(HD * (n // 2 + 8), HD), at(1024 + DEPTH * (n % 2), DEPTH)]
        slot = at((n % 4) * DEPTH, DEPTH)
        qa[...] += dot(a, kb[slot, :QR])
        kva[...] += dot_nt(a, vtb[:576, slot])
        return carry

    lax.fori_loop(0, CHUNKS, project, 0)
    fetch_rows(*c_refs(0), 4)
    for b in range(2):
        rows = slice(LOC * b, LOC * b + LOC)
        q = qa[rows, :]
        inv_q = lax.rsqrt(jnp.mean(q * q, axis=-1, keepdims=True) + EPS)
        lat[b, :, :QR] = (q * inv_q * gq[...]).astype(BF16)
        c = kva[rows, :KVR]
        inv_c = lax.rsqrt(jnp.mean(c * c, axis=-1, keepdims=True) + EPS)
        lat[b, :, QR:WID] = (c * inv_c * gkv[...]).astype(BF16)
        v1 = kva[rows, KVR:544]
        v2 = kva[rows, 544:576]
        own_cos = sb[at(NEW * b + me * LOC, LOC), :32]
        own_sin = sb[at(KVR + NEW * b + me * LOC, LOC), :32]
        rot = jnp.concatenate([v1 * own_cos - v2 * own_sin, v2 * own_cos + v1 * own_sin, jnp.zeros((LOC, LOC), F32)], axis=1)
        lat[b, :, WID:] = rot.astype(BF16)

    pl.semaphore_wait(barrier, 2)
    to_far = [remote(lat.at[b], latb.at[b, 1], lat_send.at[b, 1], lat_recv.at[b, 1], far) for b in range(2)]
    to_sib = [remote(lat.at[b], latb.at[b, 0], lat_send.at[b, 0], lat_recv.at[b, 0], sib) for b in range(2)]
    onward = [remote(latb.at[b, 1], latb.at[b, 2], lat_send.at[b, 2], lat_recv.at[b, 2], sib) for b in range(2)]
    to_far[0].start()
    to_sib[0].start()
    to_far[1].start()
    to_sib[1].start()
    fetch_wq(0)
    fetch_wq(1)
    for n in range(3):
        fetch_rows(*wo_refs(n, n), 4)
    for j in range(4):
        uk_copy(j).wait()
        wkb[HD * j:HD * j + HD, :] = kb[:WID, QR + HD * j:1664 + HD * j].reshape(HD, WID)
    for j in range(8):
        uv_copy(j).wait()
    for j in range(4):
        pair = [vtb[1024:, HD * k:HD * k + HD].reshape(LOC, WID) for k in (2 * j, 2 * j + 1)]
        wvtb[:, HD * j:HD * j + HD] = jnp.concatenate(pair, axis=0).T

    def keys_values(b, forward):
        length = len_ref[b]
        row = lax.broadcasted_iota(jnp.int32, (PREFIX, HD), 0)
        lane = lax.broadcasted_iota(jnp.int32, (PREFIX, HD), 1)
        old = row < length
        mask[...] = jnp.where(old, 1.0, 0.0).astype(BF16)
        rot = pet[b, :, :PREFIX].astype(F32).T
        rot = jnp.concatenate([rot, jnp.zeros_like(rot)], axis=1)
        pe[:PREFIX, :] = jnp.where(old, rot, jnp.where(lane == LOC, NEG, 0.0)).astype(BF16)
        pltpu.make_async_copy(*c_refs(b)).wait()

        def block(r, carry):
            if forward is not None:
                @pl.when(r == 3)
                def _():
                    forward()
            rows = at(r * ROW_BLK, ROW_BLK)
            m = mask[rows, :]
            c = cbuf[rows, :] * jnp.concatenate([m, m, m, m], axis=1)
            kb[rows, :] = dot(c, wkb[...]).astype(BF16)
            vtb[:, rows] = dot_nt(wvtb[...], c).astype(BF16)
            return carry

        lax.fori_loop(0, PREFIX // ROW_BLK, block, 0)

    def assemble(b):
        for src, owner in ((lat.at[b], me), (latb.at[b, 0], sib), (latb.at[b, 1], far), (latb.at[b, 2], diag)):
            rows = at(owner * LOC, LOC)
            lhsb[rows, :QR] = src[:, :QR]
            cn[b, rows, :] = src[:, QR:WID]
            kn[rows, :] = src[:, WID:]
        cqt[...] = lhsb[:, :QR].T
        knt[b] = kn[...].T[:LOC]
        pe[PREFIX:, :] = kn[...]
        kb[PREFIX:, :] = dot(cn[b], wkb[...]).astype(BF16)
        vtb[:, PREFIX:] = dot_nt(wvtb[...], cn[b]).astype(BF16)

    def queries(b):
        def pair(i, carry):
            @pl.when(i + 2 < 8)
            def _():
                fetch_wq(i + 2)

            pltpu.make_async_copy(*wq_refs(i)).wait()
            cos_b = cos[b]
            sin_b = sin[b]
            for k in range(2):
                q = dot(wqb[i % 3, k], cqt[...])
                v1 = q[HD:160]
                v2 = q[160:]
                qt = jnp.concatenate([q[:HD].astype(BF16), (v1 * cos_b - v2 * sin_b).astype(BF16), (v2 * cos_b + v1 * sin_b).astype(BF16), aug], axis=0)
                q_lo[2 * i + k] = qt
            return carry

        lax.fori_loop(0, 8, pair, 0)
        q_hi[0] = q_lo[0]

    def attend(b):
        halves = ((q_lo, range(5)), (q_hi, range(5, 9)))
        order = [(side, c) for c in range(5) for side, (_, blocks) in enumerate(halves) if c < len(blocks)]

        def head(h, carry):
            d = at(h * HD, HD)
            best = [jnp.full((8, NEW), NEG, F32)] * 2
            for side, k in order:
                c = halves[side][1][k]
                rows = pl.ds(c * NEW, NEW)
                s = dot(jnp.concatenate([kb[rows, d], pe[rows, :]], axis=1), halves[side][0][(h, h % 2)[side]])
                if c == 8:
                    s = jnp.where(causal, s, NEG)
                sb[rows, :] = s
                best[side] = jnp.maximum(best[side], jnp.max(s.reshape(32, 8, NEW), axis=0))
            mb[...] = jnp.maximum(*best)

            @pl.when(h >= 0)
            def _():
                m = jnp.max(mb[...], axis=0, keepdims=True) * C2
                l8 = jnp.zeros((8, NEW), F32)
                for c in range(9):
                    rows = pl.ds(c * NEW, NEW)
                    p = jnp.exp2(sb[rows, :] * C2 - m)
                    sb[rows, :] = p
                    l8 = l8 + jnp.sum(p.reshape(32, 8, NEW), axis=0)
                inv = 1.0 / jnp.sum(l8, axis=0, keepdims=True)
                acc = [jnp.zeros((HD, NEW), F32)] * 2
                for side, k in order:
                    rows = pl.ds(halves[side][1][k] * NEW, NEW)
                    acc[side] = acc[side] + dot(vtb[d, rows], (sb[rows, :] * inv).astype(BF16))
                ob[b, :, d] = (acc[0] + acc[1]).T.astype(BF16)
                q_hi[(h + 1) % 2] = q_lo[jnp.minimum(h + 1, 15)]

            return carry

        lax.fori_loop(0, 16, head, 0)

    def to_sibling(b, n):
        return remote(stage_d.at[n % 4, 0], xbuf.at[b, n], d_send.at[n % 4], d_recv.at[b, n], sib)

    def over_link(b, n):
        return remote(stage_x.at[b, n], rbuf.at[b, n], i_send.at[b, n], i_recv.at[b, n], far)

    def put_y(n):
        return pltpu.make_async_copy(ybuf.at[n % 4], y_hbm.at[:, at(n * CHUNK, CHUNK)], y_sem.at[n % 4])

    def product(rows, g, n):
        pltpu.make_async_copy(*wo_refs(g, n)).wait()
        return dot(lhsb[:rows, :], wob[g % 3])

    def next_wo(g):
        @pl.when(g + 3 < 3 * CHUNKS)
        def _():
            fetch_rows(*wo_refs(g + 3, (g + 3) % CHUNKS), 4)

    def load_lhs(k, b, owner):
        lhsb[LOC * k:LOC * k + LOC, :] = ob[b, at(owner * LOC, LOC), :]

    def far_unit(b, unit):
        load_lhs(0, b, far)
        load_lhs(1, b, diag)

        def pass_on(n):
            to_sibling(b, n).wait_recv()
            stage_x[b, n] = stage_x[b, n] + xbuf[b, n]
            over_link(b, n).start()

        def chunk(n, carry):
            g = unit * CHUNKS + n
            y = product(HD, g, n)

            @pl.when(n >= 4)
            def _():
                to_sibling(b, n - 4).wait_send()

            stage_d[n % 4, 0] = y[LOC:]
            stage_x[b, n] = y[:LOC]
            to_sibling(b, n).start()
            next_wo(g)

            @pl.when(n >= 1)
            def _():
                pass_on(n - 1)

            return carry

        lax.fori_loop(0, CHUNKS, chunk, 0)
        pass_on(CHUNKS - 1)
        for n in range(CHUNKS - 4, CHUNKS):
            to_sibling(b, n).wait_send()

    def own_unit(unit):
        for b in range(2):
            load_lhs(b, b, me)
            load_lhs(2 + b, b, sib)

        def both(n):
            return remote(stage_d.at[n % 4], xbuf.at[:, n], d_send.at[n % 4], d_recv.at[0, n], sib)

        def finish(n):
            both(n).wait_recv()

            @pl.when(n >= 4)
            def _():
                put_y(n - 4).wait()

            for b in range(2):
                over_link(b, n).wait_recv()
                total = ownb[n % 2, b] + xbuf[b, n] + rbuf[b, n]
                x = kb[at(HD * (n // 2) + LOC * b, LOC), at(CHUNK * (n % 2), CHUNK)]
                ybuf[n % 4, pl.ds(LOC * b, LOC), :] = (x.astype(F32) + total).astype(BF16)
            put_y(n).start()

        def chunk(n, carry):
            g = unit * CHUNKS + n
            y = product(NEW, g, n)

            @pl.when(n >= 4)
            def _():
                both(n - 4).wait_send()

            for b in range(2):
                ownb[n % 2, b] = y[LOC * b:LOC * b + LOC]
                stage_d[n % 4, b] = y[HD + LOC * b:192 + LOC * b]
            both(n).start()
            next_wo(g)

            @pl.when(n >= 1)
            def _():
                finish(n - 1)

            return carry

        lax.fori_loop(0, CHUNKS, chunk, 0)
        finish(CHUNKS - 1)
        for n in range(CHUNKS - 4, CHUNKS):
            both(n).wait_send()
            put_y(n).wait()

    def forward_first():
        to_far[0].wait_recv()
        onward[0].start()

    keys_values(0, forward_first)
    fetch_rows(*c_refs(1), 4)
    to_sib[0].wait_recv()
    onward[0].wait_recv()
    assemble(0)
    queries(0)
    fetch_wq(0)
    fetch_wq(1)
    attend(0)
    to_far[1].wait_recv()
    onward[1].start()
    far_unit(0, 0)
    keys_values(1, None)
    to_sib[1].wait_recv()
    onward[1].wait_recv()
    assemble(1)
    put_c = pltpu.make_async_copy(cn, cnew_hbm, out_sem.at[0])
    put_k = pltpu.make_async_copy(knt, knewt_hbm, out_sem.at[1])
    put_c.start()
    put_k.start()
    queries(1)
    attend(1)
    for j in range(7):
        x_again(j).start()
    far_unit(1, 1)
    pl.semaphore_signal(free_sem, inc=1, device_id={"tp": sib}, device_id_type=MESH)
    pl.semaphore_wait(free_sem, 1)
    for j in range(7):
        x_again(j).wait()
    own_unit(2)
    for b in range(2):
        to_far[b].wait_send()
        to_sib[b].wait_send()
        onward[b].wait_send()

        def drain(n, carry):
            over_link(b, n).wait_send()
            return carry

        lax.fori_loop(0, CHUNKS, drain, 0)
    put_c.wait()
    put_k.wait()


def main_call(lengths, *arrays):
    vmem = pl.BlockSpec(memory_space=pltpu.VMEM)
    hbm = pl.BlockSpec(memory_space=pl.ANY)
    dma = pltpu.SemaphoreType.DMA
    return pl.pallas_call(
        main_kernel,
        in_specs=[pl.BlockSpec(memory_space=pltpu.SMEM)] + [vmem] * 6 + [hbm] * 8,
        out_specs=[hbm] * 3,
        out_shape=[
            jax.ShapeDtypeStruct((HD, 7168), BF16),
            jax.ShapeDtypeStruct((2, NEW, KVR), BF16),
            jax.ShapeDtypeStruct((2, LOC, NEW), BF16),
        ],
        scratch_shapes=[
            pltpu.VMEM((2, LOC, LAT_W), BF16),
            pltpu.VMEM((HD, QR), F32),
            pltpu.VMEM((HD, 576), F32),
            pltpu.VMEM((2, 3, LOC, LAT_W), BF16),
            pltpu.VMEM((QR, NEW), BF16),
            pltpu.VMEM((2, NEW, KVR), BF16),
            pltpu.VMEM((NEW, HD), BF16),
            pltpu.VMEM((2, LOC, NEW), BF16),
            pltpu.VMEM((PREFIX + NEW, HD), BF16),
            pltpu.VMEM((PREFIX, HD), BF16),
            pltpu.VMEM((PREFIX, KVR), BF16),
            pltpu.VMEM((PREFIX + NEW, WID), BF16),
            pltpu.VMEM((WID, PREFIX + NEW), BF16),
            pltpu.VMEM((KVR, WID), BF16),
            pltpu.VMEM((WID, KVR), BF16),
            pltpu.VMEM((3, 2, 192, QR), BF16),
            pltpu.VMEM((16, NEW, NEW), BF16),
            pltpu.VMEM((2, NEW, NEW), BF16),
            pltpu.VMEM((PREFIX + NEW, NEW), F32),
            pltpu.VMEM((8, NEW), F32),
            pltpu.VMEM((2, NEW, WID), BF16),
            pltpu.VMEM((NEW, WID), BF16),
            pltpu.VMEM((3, WID, CHUNK), BF16),
            pltpu.VMEM((4, 2, LOC, CHUNK), F32),
            *[pltpu.VMEM((2, CHUNKS, LOC, CHUNK), F32)] * 3,
            pltpu.VMEM((2, 2, LOC, CHUNK), F32),
            pltpu.VMEM((4, HD, CHUNK), BF16),
            *[dma((2, 3))] * 2,
            *[dma((4,))] * 2,
            dma,
            dma((4,)),
            dma((8,)),
            dma((4,)),
            dma((3,)),
            dma((7,)),
            dma((2,)),
            dma((4,)),
            dma((4,)),
            *[dma((2, CHUNKS))] * 3,
            pltpu.SemaphoreType.REGULAR,
        ],
        compiler_params=pltpu.CompilerParams(vmem_limit_bytes=VMEM_ALL, collective_id=0, has_side_effects=True),
        cost_estimate=cost(1e11, 200 * MIB),
        name="main",
    )(lengths, *arrays)


def solution(mesh):
    def local_step(hidden, lengths, rope_cos, rope_sin, cache_lat, cache_pe, norm_in, w_dq, norm_q, w_dkv, norm_kv, w_uq, w_uk, w_uv, w_out):
        pe_t = jnp.swapaxes(cache_pe, 1, 2)
        y, c_new, k_newt = main_call(
            lengths,
            jnp.swapaxes(rope_cos, 1, 2),
            jnp.swapaxes(rope_sin, 1, 2),
            pe_t,
            norm_in[None],
            norm_q[None],
            norm_kv[None],
            hidden.reshape(HD, 7168),
            w_dq,
            w_dkv.T,
            cache_lat,
            w_uk.reshape(8192, HD),
            w_uv.reshape(8192, HD),
            jnp.transpose(w_uq, (1, 2, 0)),
            w_out,
        )
        lat_new, pe_new = update_caches(lengths, cache_lat, pe_t, c_new, k_newt)
        return y.reshape(hidden.shape), lat_new, jnp.swapaxes(pe_new, 1, 2)

    spec_tok = P("dp", "tp", None)
    spec_len = P("dp")
    spec_seq = P("dp", None, None)
    spec_vec = P(None)
    spec_mat = P(None, None)
    spec_head = P(None, "tp", None)
    spec_rows = P("tp", None)
    in_specs = (spec_tok, spec_len, spec_seq, spec_seq, spec_seq, spec_seq, spec_vec, spec_mat, spec_vec, spec_mat, spec_vec, spec_head, spec_head, spec_head, spec_rows)
    return jax.shard_map(local_step, mesh=mesh, in_specs=in_specs, out_specs=(spec_tok, spec_seq, spec_seq), check_vma=False)
```

profile of v0, /device:TPU:0, one launch (start us, length us, event | category | flops | bytes accessed | tf_op | source)
XLA Modules:
  0.0 157.6 jit_solution(4169064718236988511)
XLA Ops:
  0.6 1.3 broadcast_in_dim.10.gq
  1.9 146.9 %main.1 = (bf16[128,7168]{1,0:T(8,128)(2,1)}, bf16[2,256,512]{2,1,0:T(8,128)(2,1)}, bf16[2,64,256]{2,1,0:T(8,128)(2,1)}) custom-call(s32[2]{0:T(128)} %len_ref.3, f32[2,32,256]{2,1,0:T(8,128)} %bitcast.20, f32[2,32,256]{2,1,0:T(8,128)} %bitcast.21, bf16[2,64,2304]{2,1,0:T(8,128)(2,1)} %bitcast.18, f32[1,7168]{1,0:T(1,128)} %bitcast.22, ...), custom_call_target="tpu_custom_call" | custom-call | flops 99999997952 | bytes 209715200 | tf_op jit(solution)/shard_map/main/pallas_call | solution.py:515
  148.9 5.9 %caches.1 = (bf16[2,2304,512]{2,1,0:T(8,128)(2,1)}, bf16[2,64,2304]{2,1,0:T(8,128)(2,1)}) custom-call(s32[2]{0:T(128)} %len_ref.3, bf16[2,2304,512]{2,1,0:T(8,128)(2,1)} %c_hbm.3, bf16[2,64,2304]{2,1,0:T(8,128)(2,1)} %bitcast.19, bf16[2,256,512]{2,1,0:T(8,128)(2,1)} %get-tuple-element.9.cn_hbm, bf16[2,64,256]{2,1,0:T(8,128)(2,1)} %get-tuple-element.10.kn_hbm), custom_call_target="tpu_custom_call" | custom-call | flops 4000000000 | bytes 12582912 | tf_op jit(solution)/shard_map/caches/pallas_call | solution.py:99
  154.7 2.8 %copy.19 = bf16[2,64,7168]{2,1,0:T(8,128)(2,1)} copy(bf16[2,64,7168]{2,1,0:T(8,128)(2,1)} %bitcast.12) | data formatting | bytes 3670016
where the time goes:
time: 158 us
  Pallas kernels  153 us (97%)
  local copies, waits for them, and re-layouts  4.14 us (3%)
    pallas_call x1, Pallas kernels, main_call(): pl.pallas_call(main_kernel, in_specs=[pl.BlockSpec(memory_space=pltpu.SME...  147 us
    pallas_call x1, Pallas kernels, update_caches(): pl.pallas_call(cache_kernel, in_specs=[pl.BlockSpec(memory_space=pltpu.SM...  5.87 us

commit v1 on v0

--- a/solution.py
+++ b/solution.py
@@ -43,7 +43,7 @@
     return pl.CostEstimate(flops=int(flops), bytes_accessed=int(nbytes), transcendentals=0)
 
 
-def cache_kernel(len_ref, c_hbm, pe_hbm, cn_hbm, kn_hbm, co_hbm, po_hbm, rows, cols, cn, kn, in_sem, out_sem, side_sem):
+def cache_kernel(len_ref, y_hbm, c_hbm, pe_hbm, cn_hbm, kn_hbm, yo_hbm, co_hbm, po_hbm, y, rows, cols, cn, kn, in_sem, out_sem, side_sem, y_sem):
     blocks = rows.shape[1] // NEW
     span = lambda r: pl.ds(r * NEW, NEW)
     lat_in = lambda b, r: pltpu.make_async_copy(c_hbm.at[b, span(r)], rows.at[b, span(r)], in_sem.at[b, r])
@@ -51,6 +51,9 @@
     pe_in = lambda b: pltpu.make_async_copy(pe_hbm.at[b], cols.at[b], in_sem.at[b, blocks])
     pe_out = lambda b: pltpu.make_async_copy(cols.at[b], po_hbm.at[b], out_sem.at[b, blocks])
     new_in = [pltpu.make_async_copy(cn_hbm, cn, side_sem.at[0]), pltpu.make_async_copy(kn_hbm, kn, side_sem.at[1])]
+    part = lambda k: pl.ds(32 * k, 32)
+    y_in = [pltpu.make_async_copy(y_hbm.at[part(k)], y.at[part(k)], y_sem.at[k]) for k in range(4)]
+    y_out = [pltpu.make_async_copy(y.at[part(k)], yo_hbm.at[part(k)], y_sem.at[4 + k]) for k in range(4)]
     places = [(b, r) for b in range(2) for r in range(blocks)]
     for copy in new_in:
         copy.start()
@@ -58,6 +61,8 @@
         lat_in(b, r).start()
     for b in range(2):
         pe_in(b).start()
+    for copy in y_in:
+        copy.start()
     for copy in new_in:
         copy.wait()
     for b, r in places:
@@ -87,25 +92,30 @@
                 cols[b, :, span(r)] = jnp.where((col >= 0) & (col < NEW), dot_nt(kn[b], hot), old).astype(BF16)
 
         pe_out(b).start()
+    for k in range(4):
+        y_in[k].wait()
+        y_out[k].start()
     for b, r in places:
         lat_out(b, r).wait()
+    for copy in y_out:
+        copy.wait()
     for b in range(2):
         pe_out(b).wait()
 
 
-def update_caches(lengths, cache_lat, pe_t, c_new, k_newt):
+def update_caches(lengths, y, cache_lat, pe_t, c_new, k_newt):
     hbm = pl.BlockSpec(memory_space=pl.ANY)
     sems = pltpu.SemaphoreType.DMA((2, cache_lat.shape[1] // NEW + 1))
     return pl.pallas_call(
         cache_kernel,
-        in_specs=[pl.BlockSpec(memory_space=pltpu.SMEM)] + [hbm] * 4,
-        out_specs=[hbm] * 2,
-        out_shape=[jax.ShapeDtypeStruct(v.shape, BF16) for v in (cache_lat, pe_t)],
-        scratch_shapes=[*[pltpu.VMEM(v.shape, BF16) for v in (cache_lat, pe_t, c_new, k_newt)], sems, sems, pltpu.SemaphoreType.DMA((2,))],
+        in_specs=[pl.BlockSpec(memory_space=pltpu.SMEM)] + [hbm] * 5,
+        out_specs=[hbm] * 3,
+        out_shape=[jax.ShapeDtypeStruct(v.shape, BF16) for v in (y, cache_lat, pe_t)],
+        scratch_shapes=[*[pltpu.VMEM(v.shape, BF16) for v in (y, cache_lat, pe_t, c_new, k_newt)], sems, sems, pltpu.SemaphoreType.DMA((2,)), pltpu.SemaphoreType.DMA((8,))],
         compiler_params=pltpu.CompilerParams(vmem_limit_bytes=VMEM_ALL),
         cost_estimate=cost(4e9, 12 * MIB),
         name="caches",
-    )(lengths, cache_lat, pe_t, c_new, k_newt)
+    )(lengths, y, cache_lat, pe_t, c_new, k_newt)
 
 
 def at(start, size):
@@ -155,10 +165,10 @@
         return wdkvt_hbm.at[:, at(n * DEPTH, DEPTH)], vtb.at[pl.ds(0, 576), at((n % 4) * DEPTH, DEPTH)], dkv_sem.at[n % 4]
 
     def uk_copy(j):
-        return pltpu.make_async_copy(wuk_hbm.at[pl.ds(WID * j, WID), :], kb.at[pl.ds(0, WID), pl.ds(QR + HD * j, HD)], wk_sem.at[j])
+        return pltpu.make_async_copy(wuk_hbm.at[at(WID * j, WID), :], kb.at[pl.ds(0, WID), at(QR + HD * j, HD)], wk_sem.at[j])
 
     def uv_copy(j):
-        return pltpu.make_async_copy(wuv_hbm.at[pl.ds(1024 * j, 1024), :], vtb.at[pl.ds(1024, 1024), pl.ds(HD * j, HD)], wvt_sem.at[j])
+        return pltpu.make_async_copy(wuv_hbm.at[at(1024 * j, 1024), :], vtb.at[pl.ds(1024, 1024), at(HD * j, HD)], wvt_sem.at[j])
 
     def piece(j):
         return at(HD * (j + 8), HD), pl.ds(1024, 1024)
@@ -171,7 +181,7 @@
 
     for j in range(7):
         x_copy(j).start()
-    for n in range(3):
+    for n in range(4):
         fetch_rows(*dq_refs(n), 2)
         fetch_rows(*dkv_refs(n), 2)
 
@@ -204,7 +214,7 @@
     lax.fori_loop(0, 7, scaled, 0)
 
     def project(n, carry):
-        @pl.when(n + 3 < CHUNKS)
+        @pl.when((n >= 1) & (n + 3 < CHUNKS))
         def _():
             fetch_rows(*dq_refs(n + 3), 2)
             fetch_rows(*dkv_refs(n + 3), 2)
@@ -212,7 +222,7 @@
         pltpu.make_async_copy(*dq_refs(n)).wait()
         pltpu.make_async_copy(*dkv_refs(n)).wait()
 
-        @pl.when(n == 7)
+        @pl.when(n == 4)
         def _():
             for j in range(4):
                 uk_copy(j).start()
@@ -223,6 +233,18 @@
         slot = at((n % 4) * DEPTH, DEPTH)
         qa[...] += dot(a, kb[slot, :QR])
         kva[...] += dot_nt(a, vtb[:576, slot])
+
+        @pl.when(n >= CHUNKS - 4)
+        def _():
+            j = n - (CHUNKS - 4)
+            uk_copy(j).wait()
+            wkb[at(HD * j, HD), :] = kb[:WID, at(QR + HD * j, HD)].reshape(HD, WID)
+            halves = []
+            for k in range(2):
+                uv_copy(2 * j + k).wait()
+                halves.append(vtb[1024:WID, at(HD * (2 * j + k), HD)].reshape(LOC, WID))
+            wvtb[:, at(HD * j, HD)] = jnp.concatenate(halves, axis=0).T
+
         return carry
 
     lax.fori_loop(0, CHUNKS, project, 0)
@@ -254,16 +276,7 @@
     fetch_wq(1)
     for n in range(3):
         fetch_rows(*wo_refs(n, n), 4)
-    for j in range(4):
-        uk_copy(j).wait()
-        wkb[HD * j:HD * j + HD, :] = kb[:WID, QR + HD * j:1664 + HD * j].reshape(HD, WID)
-    for j in range(8):
-        uv_copy(j).wait()
-    for j in range(4):
-        pair = [vtb[1024:, HD * k:HD * k + HD].reshape(LOC, WID) for k in (2 * j, 2 * j + 1)]
-        wvtb[:, HD * j:HD * j + HD] = jnp.concatenate(pair, axis=0).T
-
-    def keys_values(b, forward):
+    def kv_start(b):
         length = len_ref[b]
         row = lax.broadcasted_iota(jnp.int32, (PREFIX, HD), 0)
         lane = lax.broadcasted_iota(jnp.int32, (PREFIX, HD), 1)
@@ -274,19 +287,12 @@
         pe[:PREFIX, :] = jnp.where(old, rot, jnp.where(lane == LOC, NEG, 0.0)).astype(BF16)
         pltpu.make_async_copy(*c_refs(b)).wait()
 
-        def block(r, carry):
-            if forward is not None:
-                @pl.when(r == 3)
-                def _():
-                    forward()
-            rows = at(r * ROW_BLK, ROW_BLK)
-            m = mask[rows, :]
-            c = cbuf[rows, :] * jnp.concatenate([m, m, m, m], axis=1)
-            kb[rows, :] = dot(c, wkb[...]).astype(BF16)
-            vtb[:, rows] = dot_nt(wvtb[...], c).astype(BF16)
-            return carry
-
-        lax.fori_loop(0, PREFIX // ROW_BLK, block, 0)
+    def kv_block(r):
+        rows = at(r * NEW, NEW)
+        m = mask[rows, :]
+        c = cbuf[rows, :] * jnp.concatenate([m, m, m, m], axis=1)
+        kb[rows, :] = dot(c, wkb[...]).astype(BF16)
+        vtb[:, rows] = dot_nt(wvtb[...], c).astype(BF16)
 
     def assemble(b):
         for src, owner in ((lat.at[b], me), (latb.at[b, 0], sib), (latb.at[b, 1], far), (latb.at[b, 2], diag)):
@@ -379,36 +385,34 @@
     def load_lhs(k, b, owner):
         lhsb[LOC * k:LOC * k + LOC, :] = ob[b, at(owner * LOC, LOC), :]
 
-    def far_unit(b, unit):
+    def pass_on(b, n):
+        to_sibling(b, n).wait_recv()
+        stage_x[b, n] = stage_x[b, n] + xbuf[b, n]
+        over_link(b, n).start()
+
+    def far_start(b):
         load_lhs(0, b, far)
         load_lhs(1, b, diag)
 
-        def pass_on(n):
-            to_sibling(b, n).wait_recv()
-            stage_x[b, n] = stage_x[b, n] + xbuf[b, n]
-            over_link(b, n).start()
-
-        def chunk(n, carry):
-            g = unit * CHUNKS + n
-            y = product(HD, g, n)
-
-            @pl.when(n >= 4)
-            def _():
-                to_sibling(b, n - 4).wait_send()
-
-            stage_d[n % 4, 0] = y[LOC:]
-            stage_x[b, n] = y[:LOC]
-            to_sibling(b, n).start()
-            next_wo(g)
-
-            @pl.when(n >= 1)
-            def _():
-                pass_on(n - 1)
-
-            return carry
-
-        lax.fori_loop(0, CHUNKS, chunk, 0)
-        pass_on(CHUNKS - 1)
+    def far_chunk(b, n):
+        g = b * CHUNKS + n
+        y = product(HD, g, n)
+
+        @pl.when(n >= 4)
+        def _():
+            to_sibling(b, n - 4).wait_send()
+
+        stage_d[n % 4, 0] = y[LOC:]
+        stage_x[b, n] = y[:LOC]
+        to_sibling(b, n).start()
+        next_wo(g)
+
+        @pl.when(n >= 1)
+        def _():
+            pass_on(b, n - 1)
+
+    def far_end(b):
+        pass_on(b, CHUNKS - 1)
         for n in range(CHUNKS - 4, CHUNKS):
             to_sibling(b, n).wait_send()
 
@@ -460,11 +464,30 @@
             both(n).wait_send()
             put_y(n).wait()
 
-    def forward_first():
-        to_far[0].wait_recv()
-        onward[0].start()
-
-    keys_values(0, forward_first)
+    def first_block(r, carry):
+        @pl.when(r == 6)
+        def _():
+            to_far[0].wait_recv()
+            onward[0].start()
+
+        kv_block(r)
+        return carry
+
+    def second_block(r, carry):
+        @pl.when((r >= 1) & (2 * r < CHUNKS))
+        def _():
+            far_chunk(0, 2 * r)
+            far_chunk(0, 2 * r + 1)
+
+        kv_block(r)
+        return carry
+
+    def far_only(b, n, carry):
+        far_chunk(b, n)
+        return carry
+
+    kv_start(0)
+    lax.fori_loop(0, 8, first_block, 0)
     fetch_rows(*c_refs(1), 4)
     to_sib[0].wait_recv()
     onward[0].wait_recv()
@@ -475,8 +498,11 @@
     attend(0)
     to_far[1].wait_recv()
     onward[1].start()
-    far_unit(0, 0)
-    keys_values(1, None)
+    far_start(0)
+    lax.fori_loop(0, 2, functools.partial(far_only, 0), 0)
+    kv_start(1)
+    lax.fori_loop(0, 8, second_block, 0)
+    far_end(0)
     to_sib[1].wait_recv()
     onward[1].wait_recv()
     assemble(1)
@@ -488,7 +514,9 @@
     attend(1)
     for j in range(7):
         x_again(j).start()
-    far_unit(1, 1)
+    far_start(1)
+    lax.fori_loop(0, CHUNKS, functools.partial(far_only, 1), 0)
+    far_end(1)
     pl.semaphore_signal(free_sem, inc=1, device_id={"tp": sib}, device_id_type=MESH)
     pl.semaphore_wait(free_sem, 1)
     for j in range(7):
@@ -578,7 +606,7 @@
             jnp.swapaxes(rope_sin, 1, 2),
             pe_t,
             norm_in[None],
-            norm_q[None],
+            norm_q,
             norm_kv[None],
             hidden.reshape(HD, 7168),
             w_dq,
@@ -589,7 +617,7 @@
             jnp.transpose(w_uq, (1, 2, 0)),
             w_out,
         )
-        lat_new, pe_new = update_caches(lengths, cache_lat, pe_t, c_new, k_newt)
+        y, lat_new, pe_new = update_caches(lengths, y, cache_lat, pe_t, c_new, k_newt)
         return y.reshape(hidden.shape), lat_new, jnp.swapaxes(pe_new, 1, 2)
 
     spec_tok = P("dp", "tp", None)

time: 158 us -> 157 us (level)
  local copies, waits for them, and re-layouts: 4.14 us -> 0 us
  Pallas kernels: 153 us -> 155 us
    unnamed x1 -> x0, local copies, waits for them, and re-layouts: 2.85 us -> none
where the time goes in v1:
time: 157 us; the launch traced here: 156 us
  Pallas kernels  155 us (99%)
    pallas_call x1, Pallas kernels, main_call(): pl.pallas_call(main_kernel, in_specs=[pl.BlockSpec(memory_space=pltpu.SME...  148 us
    pallas_call x1, Pallas kernels, update_caches(): pl.pallas_call(cache_kernel, in_specs=[pl.BlockSpec(memory_space=pltpu.SM...  6.93 us

profile of v1, /device:TPU:0, one launch (start us, length us, event | category | flops | bytes accessed | tf_op | source)
XLA Modules:
  0.0 156.2 jit_solution(11105570713363899006)
XLA Ops:
  0.6 148.5 %main.1 = (bf16[128,7168]{1,0:T(8,128)(2,1)}, bf16[2,256,512]{2,1,0:T(8,128)(2,1)}, bf16[2,64,256]{2,1,0:T(8,128)(2,1)}) custom-call(s32[2]{0:T(128)} %len_ref.3, f32[2,32,256]{2,1,0:T(8,128)} %bitcast.19, f32[2,32,256]{2,1,0:T(8,128)} %bitcast.20, bf16[2,64,2304]{2,1,0:T(8,128)(2,1)} %bitcast.17, f32[1,7168]{1,0:T(1,128)} %bitcast.21, f32[1536]{0:T(1024)} %gq.1, ...), custom_call_target="tpu_custom_call" | custom-call | flops 99999997952 | bytes 209715200 | tf_op jit(solution)/shard_map/main/pallas_call | solution.py:543
  149.1 6.9 %caches.1 = (bf16[128,7168]{1,0:T(8,128)(2,1)}, bf16[2,2304,512]{2,1,0:T(8,128)(2,1)}, bf16[2,64,2304]{2,1,0:T(8,128)(2,1)}) custom-call(s32[2]{0:T(128)} %len_ref.3, bf16[128,7168]{1,0:T(8,128)(2,1)} %get-tuple-element.9.y_hbm, bf16[2,2304,512]{2,1,0:T(8,128)(2,1)} %c_hbm.3, bf16[2,64,2304]{2,1,0:T(8,128)(2,1)} %bitcast.18, ...), custom_call_target="tpu_custom_call" | custom-call | flops 4000000000 | bytes 12582912 | tf_op jit(solution)/shard_map/caches/pallas_call | solution.py:109

commit v2 on v1

--- a/solution.py
+++ b/solution.py
@@ -124,10 +124,11 @@
 
 def main_kernel(len_ref, cos, sin, pet, g1, gq, gkv, x_hbm, wdq_hbm, wdkvt_hbm, c_hbm, wuk_hbm, wuv_hbm, wq_hbm, wo_hbm,
                 y_hbm, cnew_hbm, knewt_hbm,
-                lat, qa, kva, latb, cqt, cn, kn, knt, pe, mask, cbuf, kb, vtb, wkb, wvtb, wqb, q_lo, q_hi, sb, mb, ob, lhsb, wob,
-                stage_d, xbuf, stage_x, rbuf, ownb, ybuf,
+                lat, qa, kva, latb, cqt, cn, kn, knt, pe, cbuf, kb, vtb, wkb, wvtb, wqb, q_lo, q_hi, sb_a, sb_b, mb, ob, lhsb, wob,
+                stage_d, xbuf, stage_x, rbuf, ybuf,
                 lat_send, lat_recv, dq_sem, dkv_sem, c_sem, wk_sem, wvt_sem, wq_sem, wo_sem, x_sem, out_sem, y_sem,
                 d_send, d_recv, i_send, i_recv, free_sem):
+    sb = (sb_a, sb_b)
     me = lax.axis_index("tp")
     chip = me // 2
     core = me % 2
@@ -192,8 +193,8 @@
     aug = jnp.where(lax.broadcasted_iota(jnp.int32, (LOC, NEW), 0) == 0, 1.0, 0.0).astype(BF16)
     causal = lax.broadcasted_iota(jnp.int32, (NEW, NEW), 0) <= lax.broadcasted_iota(jnp.int32, (NEW, NEW), 1)
     for b in range(2):
-        sb[pl.ds(NEW * b, NEW), :32] = cos[b].T
-        sb[pl.ds(KVR + NEW * b, NEW), :32] = sin[b].T
+        sb_a[pl.ds(NEW * b, NEW), :32] = cos[b].T
+        sb_a[pl.ds(KVR + NEW * b, NEW), :32] = sin[b].T
     qa[...] = jnp.zeros_like(qa)
     kva[...] = jnp.zeros_like(kva)
     for j in range(7):
@@ -259,8 +260,8 @@
         lat[b, :, QR:WID] = (c * inv_c * gkv[...]).astype(BF16)
         v1 = kva[rows, KVR:544]
         v2 = kva[rows, 544:576]
-        own_cos = sb[at(NEW * b + me * LOC, LOC), :32]
-        own_sin = sb[at(KVR + NEW * b + me * LOC, LOC), :32]
+        own_cos = sb_a[at(NEW * b + me * LOC, LOC), :32]
+        own_sin = sb_a[at(KVR + NEW * b + me * LOC, LOC), :32]
         rot = jnp.concatenate([v1 * own_cos - v2 * own_sin, v2 * own_cos + v1 * own_sin, jnp.zeros((LOC, LOC), F32)], axis=1)
         lat[b, :, WID:] = rot.astype(BF16)
 
@@ -272,8 +273,8 @@
     to_sib[0].start()
     to_far[1].start()
     to_sib[1].start()
-    fetch_wq(0)
-    fetch_wq(1)
+    for i in range(3):
+        fetch_wq(i)
     for n in range(3):
         fetch_rows(*wo_refs(n, n), 4)
     def kv_start(b):
@@ -281,88 +282,115 @@
         row = lax.broadcasted_iota(jnp.int32, (PREFIX, HD), 0)
         lane = lax.broadcasted_iota(jnp.int32, (PREFIX, HD), 1)
         old = row < length
-        mask[...] = jnp.where(old, 1.0, 0.0).astype(BF16)
         rot = pet[b, :, :PREFIX].astype(F32).T
         rot = jnp.concatenate([rot, jnp.zeros_like(rot)], axis=1)
         pe[:PREFIX, :] = jnp.where(old, rot, jnp.where(lane == LOC, NEG, 0.0)).astype(BF16)
         pltpu.make_async_copy(*c_refs(b)).wait()
 
-    def kv_block(r):
-        rows = at(r * NEW, NEW)
-        m = mask[rows, :]
+    def kv_block(b, r, size):
+        rows = at(r * size, size)
+        row = lax.broadcasted_iota(jnp.int32, (size, HD), 0) + r * size
+        m = jnp.where(row < len_ref[b], 1.0, 0.0).astype(BF16)
         c = cbuf[rows, :] * jnp.concatenate([m, m, m, m], axis=1)
         kb[rows, :] = dot(c, wkb[...]).astype(BF16)
         vtb[:, rows] = dot_nt(wvtb[...], c).astype(BF16)
 
     def assemble(b):
+        cqa = ob.at[1]
         for src, owner in ((lat.at[b], me), (latb.at[b, 0], sib), (latb.at[b, 1], far), (latb.at[b, 2], diag)):
             rows = at(owner * LOC, LOC)
-            lhsb[rows, :QR] = src[:, :QR]
+            cqa[rows, :QR] = src[:, :QR]
             cn[b, rows, :] = src[:, QR:WID]
             kn[rows, :] = src[:, WID:]
-        cqt[...] = lhsb[:, :QR].T
+        cqt[...] = cqa[:, :QR].T
         knt[b] = kn[...].T[:LOC]
         pe[PREFIX:, :] = kn[...]
         kb[PREFIX:, :] = dot(cn[b], wkb[...]).astype(BF16)
         vtb[:, PREFIX:] = dot_nt(wvtb[...], cn[b]).astype(BF16)
 
-    def queries(b):
-        def pair(i, carry):
-            @pl.when(i + 2 < 8)
-            def _():
-                fetch_wq(i + 2)
-
-            pltpu.make_async_copy(*wq_refs(i)).wait()
-            cos_b = cos[b]
-            sin_b = sin[b]
-            for k in range(2):
-                q = dot(wqb[i % 3, k], cqt[...])
-                v1 = q[HD:160]
-                v2 = q[160:]
-                qt = jnp.concatenate([q[:HD].astype(BF16), (v1 * cos_b - v2 * sin_b).astype(BF16), (v2 * cos_b + v1 * sin_b).astype(BF16), aug], axis=0)
-                q_lo[2 * i + k] = qt
-            return carry
-
-        lax.fori_loop(0, 8, pair, 0)
-        q_hi[0] = q_lo[0]
+    def query_pair(b, i):
+        pltpu.make_async_copy(*wq_refs(i)).wait()
+        cos_b = cos[b]
+        sin_b = sin[b]
+        for k in range(2):
+            q = dot(wqb[i % 3, k], cqt[...])
+            v1 = q[HD:160]
+            v2 = q[160:]
+            qt = jnp.concatenate([q[:HD].astype(BF16), (v1 * cos_b - v2 * sin_b).astype(BF16), (v2 * cos_b + v1 * sin_b).astype(BF16), aug], axis=0)
+            q_lo[2 * i + k] = qt
+
+        @pl.when(i + 3 < 8)
+        def _():
+            fetch_wq(i + 3)
+
+    def first_queries(i, carry):
+        query_pair(0, i)
+        return carry
 
     def attend(b):
         halves = ((q_lo, range(5)), (q_hi, range(5, 9)))
         order = [(side, c) for c in range(5) for side, (_, blocks) in enumerate(halves) if c < len(blocks)]
 
-        def head(h, carry):
+        def score(h, k):
             d = at(h * HD, HD)
             best = [jnp.full((8, NEW), NEG, F32)] * 2
-            for side, k in order:
-                c = halves[side][1][k]
+            for side, j in order:
+                c = halves[side][1][j]
                 rows = pl.ds(c * NEW, NEW)
-                s = dot(jnp.concatenate([kb[rows, d], pe[rows, :]], axis=1), halves[side][0][(h, h % 2)[side]])
+                t = dot(jnp.concatenate([kb[rows, d], pe[rows, :]], axis=1), halves[side][0][(h, k)[side]])
                 if c == 8:
-                    s = jnp.where(causal, s, NEG)
-                sb[rows, :] = s
-                best[side] = jnp.maximum(best[side], jnp.max(s.reshape(32, 8, NEW), axis=0))
-            mb[...] = jnp.maximum(*best)
-
-            @pl.when(h >= 0)
+                    t = jnp.where(causal, t, NEG)
+                sb[k][rows, :] = t
+                best[side] = jnp.maximum(best[side], jnp.max(t.reshape(32, 8, NEW), axis=0))
+                yield
+            mb[k] = jnp.maximum(*best)
+
+        def finish(h, k):
+            d = at(h * HD, HD)
+            m = jnp.max(mb[k], axis=0, keepdims=True) * C2
+            l8 = jnp.zeros((8, NEW), F32)
+            for c in range(9):
+                rows = pl.ds(c * NEW, NEW)
+                p = jnp.exp2(sb[k][rows, :] * C2 - m)
+                sb[k][rows, :] = p
+                l8 = l8 + jnp.sum(p.reshape(32, 8, NEW), axis=0)
+                yield
+            inv = 1.0 / jnp.sum(l8, axis=0, keepdims=True)
+            acc = [jnp.zeros((HD, NEW), F32)] * 2
+            for side, j in order:
+                rows = pl.ds(halves[side][1][j] * NEW, NEW)
+                acc[side] = acc[side] + dot(vtb[d, rows], (sb[k][rows, :] * inv).astype(BF16))
+                yield
+            ob[b, :, d] = (acc[0] + acc[1]).T.astype(BF16)
+
+        def weave(*parts):
+            live = list(parts)
+            while live:
+                live = [part for part in live if next(part, live) is None]
+
+        for k in range(2):
+            q_hi[k] = q_lo[k]
+
+        @pl.when(me >= 0)
+        def _():
+            weave(score(0, 0))
+
+        def pair(i, carry):
+            h = 2 * i
+
+            @pl.when(i >= 0)
             def _():
-                m = jnp.max(mb[...], axis=0, keepdims=True) * C2
-                l8 = jnp.zeros((8, NEW), F32)
-                for c in range(9):
-                    rows = pl.ds(c * NEW, NEW)
-                    p = jnp.exp2(sb[rows, :] * C2 - m)
-                    sb[rows, :] = p
-                    l8 = l8 + jnp.sum(p.reshape(32, 8, NEW), axis=0)
-                inv = 1.0 / jnp.sum(l8, axis=0, keepdims=True)
-                acc = [jnp.zeros((HD, NEW), F32)] * 2
-                for side, k in order:
-                    rows = pl.ds(halves[side][1][k] * NEW, NEW)
-                    acc[side] = acc[side] + dot(vtb[d, rows], (sb[rows, :] * inv).astype(BF16))
-                ob[b, :, d] = (acc[0] + acc[1]).T.astype(BF16)
-                q_hi[(h + 1) % 2] = q_lo[jnp.minimum(h + 1, 15)]
+                weave(score(h + 1, 1), finish(h, 0))
+                q_hi[0] = q_lo[jnp.minimum(h + 2, 15)]
+
+            @pl.when(i < 8)
+            def _():
+                weave(score(jnp.minimum(h + 2, 15), 0), finish(h + 1, 1))
+                q_hi[1] = q_lo[jnp.minimum(h + 3, 15)]
 
             return carry
 
-        lax.fori_loop(0, 16, head, 0)
+        lax.fori_loop(0, 8, pair, 0)
 
     def to_sibling(b, n):
         return remote(stage_d.at[n % 4, 0], xbuf.at[b, n], d_send.at[n % 4], d_recv.at[b, n], sib)
@@ -407,16 +435,23 @@
         to_sibling(b, n).start()
         next_wo(g)
 
-        @pl.when(n >= 1)
-        def _():
-            pass_on(b, n - 1)
+        @pl.when(n == 1)
+        def _():
+            pass_on(b, 0)
+
+        @pl.when(n >= 3)
+        def _():
+            pass_on(b, n - 2)
 
     def far_end(b):
+        pass_on(b, CHUNKS - 2)
         pass_on(b, CHUNKS - 1)
         for n in range(CHUNKS - 4, CHUNKS):
             to_sibling(b, n).wait_send()
 
     def own_unit(unit):
+        for n in range(4):
+            over_link(0, n).wait_send()
         for b in range(2):
             load_lhs(b, b, me)
             load_lhs(2 + b, b, sib)
@@ -433,7 +468,7 @@
 
             for b in range(2):
                 over_link(b, n).wait_recv()
-                total = ownb[n % 2, b] + xbuf[b, n] + rbuf[b, n]
+                total = stage_x[0, 2 * (n % 2) + b] + xbuf[b, n] + rbuf[b, n]
                 x = kb[at(HD * (n // 2) + LOC * b, LOC), at(CHUNK * (n % 2), CHUNK)]
                 ybuf[n % 4, pl.ds(LOC * b, LOC), :] = (x.astype(F32) + total).astype(BF16)
             put_y(n).start()
@@ -447,7 +482,7 @@
                 both(n - 4).wait_send()
 
             for b in range(2):
-                ownb[n % 2, b] = y[LOC * b:LOC * b + LOC]
+                stage_x[0, 2 * (n % 2) + b] = y[LOC * b:LOC * b + LOC]
                 stage_d[n % 4, b] = y[HD + LOC * b:192 + LOC * b]
             both(n).start()
             next_wo(g)
@@ -465,12 +500,12 @@
             put_y(n).wait()
 
     def first_block(r, carry):
-        @pl.when(r == 6)
+        @pl.when(r == 3)
         def _():
             to_far[0].wait_recv()
             onward[0].start()
 
-        kv_block(r)
+        kv_block(0, r, ROW_BLK)
         return carry
 
     def second_block(r, carry):
@@ -479,7 +514,8 @@
             far_chunk(0, 2 * r)
             far_chunk(0, 2 * r + 1)
 
-        kv_block(r)
+        kv_block(1, r, NEW)
+        query_pair(1, r)
         return carry
 
     def far_only(b, n, carry):
@@ -487,30 +523,29 @@
         return carry
 
     kv_start(0)
-    lax.fori_loop(0, 8, first_block, 0)
+    lax.fori_loop(0, PREFIX // ROW_BLK, first_block, 0)
     fetch_rows(*c_refs(1), 4)
     to_sib[0].wait_recv()
     onward[0].wait_recv()
     assemble(0)
-    queries(0)
-    fetch_wq(0)
-    fetch_wq(1)
+    lax.fori_loop(0, 8, first_queries, 0)
+    for i in range(3):
+        fetch_wq(i)
     attend(0)
     to_far[1].wait_recv()
     onward[1].start()
     far_start(0)
     lax.fori_loop(0, 2, functools.partial(far_only, 0), 0)
     kv_start(1)
-    lax.fori_loop(0, 8, second_block, 0)
-    far_end(0)
     to_sib[1].wait_recv()
     onward[1].wait_recv()
     assemble(1)
+    lax.fori_loop(0, 8, second_block, 0)
+    far_end(0)
     put_c = pltpu.make_async_copy(cn, cnew_hbm, out_sem.at[0])
     put_k = pltpu.make_async_copy(knt, knewt_hbm, out_sem.at[1])
     put_c.start()
     put_k.start()
-    queries(1)
     attend(1)
     for j in range(7):
         x_again(j).start()
@@ -531,7 +566,7 @@
             over_link(b, n).wait_send()
             return carry
 
-        lax.fori_loop(0, CHUNKS, drain, 0)
+        lax.fori_loop((4, 0)[b], CHUNKS, drain, 0)
     put_c.wait()
     put_k.wait()
 
@@ -559,7 +594,6 @@
             pltpu.VMEM((NEW, HD), BF16),
             pltpu.VMEM((2, LOC, NEW), BF16),
             pltpu.VMEM((PREFIX + NEW, HD), BF16),
-            pltpu.VMEM((PREFIX, HD), BF16),
             pltpu.VMEM((PREFIX, KVR), BF16),
             pltpu.VMEM((PREFIX + NEW, WID), BF16),
             pltpu.VMEM((WID, PREFIX + NEW), BF16),
@@ -568,14 +602,13 @@
             pltpu.VMEM((3, 2, 192, QR), BF16),
             pltpu.VMEM((16, NEW, NEW), BF16),
             pltpu.VMEM((2, NEW, NEW), BF16),
-            pltpu.VMEM((PREFIX + NEW, NEW), F32),
-            pltpu.VMEM((8, NEW), F32),
+            *[pltpu.VMEM((PREFIX + NEW, NEW), F32)] * 2,
+            pltpu.VMEM((2, 8, NEW), F32),
             pltpu.VMEM((2, NEW, WID), BF16),
             pltpu.VMEM((NEW, WID), BF16),
             pltpu.VMEM((3, WID, CHUNK), BF16),
             pltpu.VMEM((4, 2, LOC, CHUNK), F32),
             *[pltpu.VMEM((2, CHUNKS, LOC, CHUNK), F32)] * 3,
-            pltpu.VMEM((2, 2, LOC, CHUNK), F32),
             pltpu.VMEM((4, HD, CHUNK), BF16),
             *[dma((2, 3))] * 2,
             *[dma((4,))] * 2,

time: 157 us -> 150 us (0.955)
  Pallas kernels: 155 us -> 149 us
    pallas_call x1, Pallas kernels: 148 us -> 142 us  [main_call(): pl.pallas_call(main_kernel, in_specs=[pl.BlockSpec(memory_space=pltpu.SME...]
where the time goes in v2:
time: 150 us
  Pallas kernels  149 us (99%)
    pallas_call x1, Pallas kernels, main_call(): pl.pallas_call(main_kernel, in_specs=[pl.BlockSpec(memory_space=pltpu.SME...  142 us
    pallas_call x1, Pallas kernels, update_caches(): pl.pallas_call(cache_kernel, in_specs=[pl.BlockSpec(memory_space=pltpu.SM...  6.93 us

profile of v2, /device:TPU:0, one launch (start us, length us, event | category | flops | bytes accessed | tf_op | source)
XLA Modules:
  0.0 149.9 jit_solution(6361766221879018312)
XLA Ops:
  0.6 142.2 %main.1 = (bf16[128,7168]{1,0:T(8,128)(2,1)}, bf16[2,256,512]{2,1,0:T(8,128)(2,1)}, bf16[2,64,256]{2,1,0:T(8,128)(2,1)}) custom-call(s32[2]{0:T(128)} %len_ref.3, f32[2,32,256]{2,1,0:T(8,128)} %bitcast.19, f32[2,32,256]{2,1,0:T(8,128)} %bitcast.20, bf16[2,64,2304]{2,1,0:T(8,128)(2,1)} %bitcast.17, f32[1,7168]{1,0:T(1,128)} %bitcast.21, f32[1536]{0:T(1024)} %gq.1, ...), custom_call_target="tpu_custom_call" | custom-call | flops 99999997952 | bytes 209715200 | tf_op jit(solution)/shard_map/main/pallas_call | solution.py:578
  142.8 6.9 %caches.1 = (bf16[128,7168]{1,0:T(8,128)(2,1)}, bf16[2,2304,512]{2,1,0:T(8,128)(2,1)}, bf16[2,64,2304]{2,1,0:T(8,128)(2,1)}) custom-call(s32[2]{0:T(128)} %len_ref.3, bf16[128,7168]{1,0:T(8,128)(2,1)} %get-tuple-element.9.y_hbm, bf16[2,2304,512]{2,1,0:T(8,128)(2,1)} %c_hbm.3, bf16[2,64,2304]{2,1,0:T(8,128)(2,1)} %bitcast.18, ...), custom_call_target="tpu_custom_call" | custom-call | flops 4000000000 | bytes 12582912 | tf_op jit(solution)/shard_map/caches/pallas_call | solution.py:109

commit v3 on v2

--- a/solution.py
+++ b/solution.py
@@ -235,6 +235,10 @@
         qa[...] += dot(a, kb[slot, :QR])
         kva[...] += dot_nt(a, vtb[:576, slot])
 
+        @pl.when(n == CHUNKS - 3)
+        def _():
+            fetch_rows(*c_refs(0), 4)
+
         @pl.when(n >= CHUNKS - 4)
         def _():
             j = n - (CHUNKS - 4)
@@ -249,7 +253,6 @@
         return carry
 
     lax.fori_loop(0, CHUNKS, project, 0)
-    fetch_rows(*c_refs(0), 4)
     for b in range(2):
         rows = slice(LOC * b, LOC * b + LOC)
         q = qa[rows, :]
@@ -271,7 +274,6 @@
     onward = [remote(latb.at[b, 1], latb.at[b, 2], lat_send.at[b, 2], lat_recv.at[b, 2], sib) for b in range(2)]
     to_far[0].start()
     to_sib[0].start()
-    to_far[1].start()
     to_sib[1].start()
     for i in range(3):
         fetch_wq(i)
@@ -313,7 +315,7 @@
         cos_b = cos[b]
         sin_b = sin[b]
         for k in range(2):
-            q = dot(wqb[i % 3, k], cqt[...])
+            q = dot(wqb[i % 3, k, :, :CB], cqt[:CB, :]) + dot(wqb[i % 3, k, :, CB:], cqt[CB:, :])
             v1 = q[HD:160]
             v2 = q[160:]
             qt = jnp.concatenate([q[:HD].astype(BF16), (v1 * cos_b - v2 * sin_b).astype(BF16), (v2 * cos_b + v1 * sin_b).astype(BF16), aug], axis=0)
@@ -323,11 +325,10 @@
         def _():
             fetch_wq(i + 3)
 
-    def first_queries(i, carry):
-        query_pair(0, i)
-        return carry
-
-    def attend(b):
+    def attend(b, inside):
+        if inside:
+            query_pair(b, jnp.int32(0))
+
         halves = ((q_lo, range(5)), (q_hi, range(5, 9)))
         order = [(side, c) for c in range(5) for side, (_, blocks) in enumerate(halves) if c < len(blocks)]
 
@@ -377,6 +378,10 @@
 
         def pair(i, carry):
             h = 2 * i
+            if inside:
+                @pl.when(i < 7)
+                def _():
+                    query_pair(b, i + 1)
 
             @pl.when(i >= 0)
             def _():
@@ -502,6 +507,7 @@
     def first_block(r, carry):
         @pl.when(r == 3)
         def _():
+            to_far[1].start()
             to_far[0].wait_recv()
             onward[0].start()
 
@@ -509,13 +515,13 @@
         return carry
 
     def second_block(r, carry):
-        @pl.when((r >= 1) & (2 * r < CHUNKS))
-        def _():
-            far_chunk(0, 2 * r)
-            far_chunk(0, 2 * r + 1)
-
-        kv_block(1, r, NEW)
-        query_pair(1, r)
+        n = 3 * r + 2
+        far_chunk(0, n)
+        query_pair(1, 2 * r)
+        far_chunk(0, n + 1)
+        query_pair(1, 2 * r + 1)
+        far_chunk(0, n + 2)
+        kv_block(1, r, ROW_BLK)
         return carry
 
     def far_only(b, n, carry):
@@ -528,10 +534,9 @@
     to_sib[0].wait_recv()
     onward[0].wait_recv()
     assemble(0)
-    lax.fori_loop(0, 8, first_queries, 0)
+    attend(0, True)
     for i in range(3):
         fetch_wq(i)
-    attend(0)
     to_far[1].wait_recv()
     onward[1].start()
     far_start(0)
@@ -540,13 +545,13 @@
     to_sib[1].wait_recv()
     onward[1].wait_recv()
     assemble(1)
-    lax.fori_loop(0, 8, second_block, 0)
+    lax.fori_loop(0, PREFIX // ROW_BLK, second_block, 0)
     far_end(0)
     put_c = pltpu.make_async_copy(cn, cnew_hbm, out_sem.at[0])
     put_k = pltpu.make_async_copy(knt, knewt_hbm, out_sem.at[1])
     put_c.start()
     put_k.start()
-    attend(1)
+    attend(1, False)
     for j in range(7):
         x_again(j).start()
     far_start(1)

time: 150 us -> 144 us (0.960)
  Pallas kernels: 149 us -> 143 us
    pallas_call x1, Pallas kernels: 142 us -> 136 us  [main_call(): pl.pallas_call(main_kernel, in_specs=[pl.BlockSpec(memory_space=pltpu.SME...]
where the time goes in v3:
time: 144 us
  Pallas kernels  143 us (99%)
    pallas_call x1, Pallas kernels, main_call(): pl.pallas_call(main_kernel, in_specs=[pl.BlockSpec(memory_space=pltpu.SME...  136 us
    pallas_call x1, Pallas kernels, update_caches(): pl.pallas_call(cache_kernel, in_specs=[pl.BlockSpec(memory_space=pltpu.SM...  7.1 us

profile of v3, /device:TPU:0, one launch (start us, length us, event | category | flops | bytes accessed | tf_op | source)
XLA Modules:
  0.0 144.2 jit_solution(11938771894131915586)
XLA Ops:
  0.6 136.2 %main.1 = (bf16[128,7168]{1,0:T(8,128)(2,1)}, bf16[2,256,512]{2,1,0:T(8,128)(2,1)}, bf16[2,64,256]{2,1,0:T(8,128)(2,1)}) custom-call(s32[2]{0:T(128)} %len_ref.3, f32[2,32,256]{2,1,0:T(8,128)} %bitcast.19, f32[2,32,256]{2,1,0:T(8,128)} %bitcast.20, bf16[2,64,2304]{2,1,0:T(8,128)(2,1)} %bitcast.17, f32[1,7168]{1,0:T(1,128)} %bitcast.21, f32[1536]{0:T(1024)} %gq.1, ...), custom_call_target="tpu_custom_call" | custom-call | flops 99999997952 | bytes 209715200 | tf_op jit(solution)/shard_map/main/pallas_call | solution.py:583
  136.9 7.1 %caches.1 = (bf16[128,7168]{1,0:T(8,128)(2,1)}, bf16[2,2304,512]{2,1,0:T(8,128)(2,1)}, bf16[2,64,2304]{2,1,0:T(8,128)(2,1)}) custom-call(s32[2]{0:T(128)} %len_ref.3, bf16[128,7168]{1,0:T(8,128)(2,1)} %get-tuple-element.9.y_hbm, bf16[2,2304,512]{2,1,0:T(8,128)(2,1)} %c_hbm.3, bf16[2,64,2304]{2,1,0:T(8,128)(2,1)} %bitcast.18, ...), custom_call_target="tpu_custom_call" | custom-call | flops 4000000000 | bytes 12582912 | tf_op jit(solution)/shard_map/caches/pallas_call | solution.py:109

commit v4 on v3

--- a/solution.py
+++ b/solution.py
@@ -310,8 +310,7 @@
         kb[PREFIX:, :] = dot(cn[b], wkb[...]).astype(BF16)
         vtb[:, PREFIX:] = dot_nt(wvtb[...], cn[b]).astype(BF16)
 
-    def query_pair(b, i):
-        pltpu.make_async_copy(*wq_refs(i)).wait()
+    def query(b, i):
         cos_b = cos[b]
         sin_b = sin[b]
         for k in range(2):
@@ -320,15 +319,19 @@
             v2 = q[160:]
             qt = jnp.concatenate([q[:HD].astype(BF16), (v1 * cos_b - v2 * sin_b).astype(BF16), (v2 * cos_b + v1 * sin_b).astype(BF16), aug], axis=0)
             q_lo[2 * i + k] = qt
-
-        @pl.when(i + 3 < 8)
-        def _():
-            fetch_wq(i + 3)
-
-    def attend(b, inside):
-        if inside:
-            query_pair(b, jnp.int32(0))
-
+            if k == 0:
+                q_hi[0] = qt
+            yield
+
+    def attend(b):
+        def weave(*parts):
+            live = list(parts)
+            while live:
+                live = [part for part in live if next(part, live) is None]
+
+        pltpu.make_async_copy(*wq_refs(0)).wait()
+        weave(query(b, jnp.int32(0)))
+        fetch_wq(3)
         halves = ((q_lo, range(5)), (q_hi, range(5, 9)))
         order = [(side, c) for c in range(5) for side, (_, blocks) in enumerate(halves) if c < len(blocks)]
 
@@ -364,35 +367,27 @@
                 yield
             ob[b, :, d] = (acc[0] + acc[1]).T.astype(BF16)
 
-        def weave(*parts):
-            live = list(parts)
-            while live:
-                live = [part for part in live if next(part, live) is None]
-
-        for k in range(2):
-            q_hi[k] = q_lo[k]
-
         @pl.when(me >= 0)
         def _():
             weave(score(0, 0))
+            q_hi[1] = q_lo[1]
 
         def pair(i, carry):
             h = 2 * i
-            if inside:
-                @pl.when(i < 7)
-                def _():
-                    query_pair(b, i + 1)
-
-            @pl.when(i >= 0)
+            later = jnp.minimum(i + 1, 7)
+
+            @pl.when(i < 7)
             def _():
-                weave(score(h + 1, 1), finish(h, 0))
-                q_hi[0] = q_lo[jnp.minimum(h + 2, 15)]
-
-            @pl.when(i < 8)
+                pltpu.make_async_copy(*wq_refs(i + 1)).wait()
+
+            weave(score(h + 1, 1), finish(h, 0), query(b, later))
+
+            @pl.when(i + 4 < 8)
             def _():
-                weave(score(jnp.minimum(h + 2, 15), 0), finish(h + 1, 1))
-                q_hi[1] = q_lo[jnp.minimum(h + 3, 15)]
-
+                fetch_wq(i + 4)
+
+            weave(score(2 * later, 0), finish(h + 1, 1))
+            q_hi[1] = q_lo[2 * later + 1]
             return carry
 
         lax.fori_loop(0, 8, pair, 0)
@@ -517,9 +512,7 @@
     def second_block(r, carry):
         n = 3 * r + 2
         far_chunk(0, n)
-        query_pair(1, 2 * r)
         far_chunk(0, n + 1)
-        query_pair(1, 2 * r + 1)
         far_chunk(0, n + 2)
         kv_block(1, r, ROW_BLK)
         return carry
@@ -534,7 +527,7 @@
     to_sib[0].wait_recv()
     onward[0].wait_recv()
     assemble(0)
-    attend(0, True)
+    attend(0)
     for i in range(3):
         fetch_wq(i)
     to_far[1].wait_recv()
@@ -551,7 +544,7 @@
     put_k = pltpu.make_async_copy(knt, knewt_hbm, out_sem.at[1])
     put_c.start()
     put_k.start()
-    attend(1, False)
+    attend(1)
     for j in range(7):
         x_again(j).start()
     far_start(1)

time: 144 us -> 145 us (level)
  no operation moved by 1% of the time
where the time goes in v4:
time: 145 us; the launch traced here: 144 us
  Pallas kernels  144 us (99%)
    pallas_call x1, Pallas kernels, main_call(): pl.pallas_call(main_kernel, in_specs=[pl.BlockSpec(memory_space=pltpu.SME...  137 us
    pallas_call x1, Pallas kernels, update_caches(): pl.pallas_call(cache_kernel, in_specs=[pl.BlockSpec(memory_space=pltpu.SM...  7.04 us

profile of v4, /device:TPU:0, one launch (start us, length us, event | category | flops | bytes accessed | tf_op | source)
XLA Modules:
  0.0 144.4 jit_solution(7310442765930424316)
XLA Ops:
  0.6 136.6 %main.1 = (bf16[128,7168]{1,0:T(8,128)(2,1)}, bf16[2,256,512]{2,1,0:T(8,128)(2,1)}, bf16[2,64,256]{2,1,0:T(8,128)(2,1)}) custom-call(s32[2]{0:T(128)} %len_ref.3, f32[2,32,256]{2,1,0:T(8,128)} %bitcast.19, f32[2,32,256]{2,1,0:T(8,128)} %bitcast.20, bf16[2,64,2304]{2,1,0:T(8,128)(2,1)} %bitcast.17, f32[1,7168]{1,0:T(1,128)} %bitcast.21, f32[1536]{0:T(1024)} %gq.1, ...), custom_call_target="tpu_custom_call" | custom-call | flops 99999997952 | bytes 209715200 | tf_op jit(solution)/shard_map/main/pallas_call | solution.py:576
  137.2 7.0 %caches.1 = (bf16[128,7168]{1,0:T(8,128)(2,1)}, bf16[2,2304,512]{2,1,0:T(8,128)(2,1)}, bf16[2,64,2304]{2,1,0:T(8,128)(2,1)}) custom-call(s32[2]{0:T(128)} %len_ref.3, bf16[128,7168]{1,0:T(8,128)(2,1)} %get-tuple-element.9.y_hbm, bf16[2,2304,512]{2,1,0:T(8,128)(2,1)} %c_hbm.3, bf16[2,64,2304]{2,1,0:T(8,128)(2,1)} %bitcast.18, ...), custom_call_target="tpu_custom_call" | custom-call | flops 4000000000 | bytes 12582912 | tf_op jit(solution)/shard_map/caches/pallas_call | solution.py:109

commit v5 on v3

--- a/solution.py
+++ b/solution.py
@@ -57,14 +57,17 @@
     places = [(b, r) for b in range(2) for r in range(blocks)]
     for copy in new_in:
         copy.start()
+    for copy in y_in:
+        copy.start()
     for b, r in places:
         lat_in(b, r).start()
     for b in range(2):
         pe_in(b).start()
-    for copy in y_in:
-        copy.start()
     for copy in new_in:
         copy.wait()
+    for k in range(4):
+        y_in[k].wait()
+        y_out[k].start()
     for b, r in places:
         shift = r * NEW - len_ref[b]
         lat_in(b, r).wait()
@@ -92,9 +95,6 @@
                 cols[b, :, span(r)] = jnp.where((col >= 0) & (col < NEW), dot_nt(kn[b], hot), old).astype(BF16)
 
         pe_out(b).start()
-    for k in range(4):
-        y_in[k].wait()
-        y_out[k].start()
     for b, r in places:
         lat_out(b, r).wait()
     for copy in y_out:
@@ -338,7 +338,7 @@
             for side, j in order:
                 c = halves[side][1][j]
                 rows = pl.ds(c * NEW, NEW)
-                t = dot(jnp.concatenate([kb[rows, d], pe[rows, :]], axis=1), halves[side][0][(h, k)[side]])
+                t = dot(jnp.concatenate([kb[rows, d], pe[rows, :]], axis=1), halves[side][0][(h, k)[side]]) * C2
                 if c == 8:
                     t = jnp.where(causal, t, NEG)
                 sb[k][rows, :] = t
@@ -348,11 +348,11 @@
 
         def finish(h, k):
             d = at(h * HD, HD)
-            m = jnp.max(mb[k], axis=0, keepdims=True) * C2
+            m = jnp.max(mb[k], axis=0, keepdims=True)
             l8 = jnp.zeros((8, NEW), F32)
             for c in range(9):
                 rows = pl.ds(c * NEW, NEW)
-                p = jnp.exp2(sb[k][rows, :] * C2 - m)
+                p = jnp.exp2(sb[k][rows, :] - m)
                 sb[k][rows, :] = p
                 l8 = l8 + jnp.sum(p.reshape(32, 8, NEW), axis=0)
                 yield

time: 144 us -> 143 us (level)
    pallas_call x1, Pallas kernels: 136 us -> 135 us  [main_call(): pl.pallas_call(main_kernel, in_specs=[pl.BlockSpec(memory_space=pltpu.SME...]
where the time goes in v5:
time: 143 us
  Pallas kernels  142 us (99%)
    pallas_call x1, Pallas kernels, main_call(): pl.pallas_call(main_kernel, in_specs=[pl.BlockSpec(memory_space=pltpu.SME...  135 us
    pallas_call x1, Pallas kernels, update_caches(): pl.pallas_call(cache_kernel, in_specs=[pl.BlockSpec(memory_space=pltpu.SM...  6.93 us

profile of v5, /device:TPU:0, one launch (start us, length us, event | category | flops | bytes accessed | tf_op | source)
XLA Modules:
  0.0 142.5 jit_solution(6787273797561600767)
XLA Ops:
  0.6 134.8 %main.1 = (bf16[128,7168]{1,0:T(8,128)(2,1)}, bf16[2,256,512]{2,1,0:T(8,128)(2,1)}, bf16[2,64,256]{2,1,0:T(8,128)(2,1)}) custom-call(s32[2]{0:T(128)} %len_ref.3, f32[2,32,256]{2,1,0:T(8,128)} %bitcast.19, f32[2,32,256]{2,1,0:T(8,128)} %bitcast.20, bf16[2,64,2304]{2,1,0:T(8,128)(2,1)} %bitcast.17, f32[1,7168]{1,0:T(1,128)} %bitcast.21, f32[1536]{0:T(1024)} %gq.1, ...), custom_call_target="tpu_custom_call" | custom-call | flops 99999997952 | bytes 209715200 | tf_op jit(solution)/shard_map/main/pallas_call | solution.py:583
  135.4 6.9 %caches.1 = (bf16[128,7168]{1,0:T(8,128)(2,1)}, bf16[2,2304,512]{2,1,0:T(8,128)(2,1)}, bf16[2,64,2304]{2,1,0:T(8,128)(2,1)}) custom-call(s32[2]{0:T(128)} %len_ref.3, bf16[128,7168]{1,0:T(8,128)(2,1)} %get-tuple-element.9.y_hbm, bf16[2,2304,512]{2,1,0:T(8,128)(2,1)} %c_hbm.3, bf16[2,64,2304]{2,1,0:T(8,128)(2,1)} %bitcast.18, ...), custom_call_target="tpu_custom_call" | custom-call | flops 4000000000 | bytes 12582912 | tf_op jit(solution)/shard_map/caches/pallas_call | solution.py:109

commit v6 on v5

--- a/solution.py
+++ b/solution.py
@@ -185,6 +185,10 @@
     for n in range(4):
         fetch_rows(*dq_refs(n), 2)
         fetch_rows(*dkv_refs(n), 2)
+    for j in range(4):
+        uk_copy(j).start()
+    for j in range(8):
+        uv_copy(j).start()
 
     barrier = pltpu.get_barrier_semaphore()
     for peer in (sib, far):
@@ -222,13 +226,6 @@
 
         pltpu.make_async_copy(*dq_refs(n)).wait()
         pltpu.make_async_copy(*dkv_refs(n)).wait()
-
-        @pl.when(n == 4)
-        def _():
-            for j in range(4):
-                uk_copy(j).start()
-            for j in range(8):
-                uv_copy(j).start()
 
         a = vtb[at(HD * (n // 2 + 8), HD), at(1024 + DEPTH * (n % 2), DEPTH)]
         slot = at((n % 4) * DEPTH, DEPTH)

time: 143 us -> 143 us (level)
  no operation moved by 1% of the time
where the time goes in v6:
time: 143 us; the launch traced here: 142 us
  Pallas kernels  142 us (99%)
    pallas_call x1, Pallas kernels, main_call(): pl.pallas_call(main_kernel, in_specs=[pl.BlockSpec(memory_space=pltpu.SME...  135 us
    pallas_call x1, Pallas kernels, update_caches(): pl.pallas_call(cache_kernel, in_specs=[pl.BlockSpec(memory_space=pltpu.SM...  6.93 us

profile of v6, /device:TPU:0, one launch (start us, length us, event | category | flops | bytes accessed | tf_op | source)
XLA Modules:
  0.0 142.4 jit_solution(17416110469343859066)
XLA Ops:
  0.6 134.6 %main.1 = (bf16[128,7168]{1,0:T(8,128)(2,1)}, bf16[2,256,512]{2,1,0:T(8,128)(2,1)}, bf16[2,64,256]{2,1,0:T(8,128)(2,1)}) custom-call(s32[2]{0:T(128)} %len_ref.3, f32[2,32,256]{2,1,0:T(8,128)} %bitcast.19, f32[2,32,256]{2,1,0:T(8,128)} %bitcast.20, bf16[2,64,2304]{2,1,0:T(8,128)(2,1)} %bitcast.17, f32[1,7168]{1,0:T(1,128)} %bitcast.21, f32[1536]{0:T(1024)} %gq.1, ...), custom_call_target="tpu_custom_call" | custom-call | flops 99999997952 | bytes 209715200 | tf_op jit(solution)/shard_map/main/pallas_call | solution.py:580
  135.3 6.9 %caches.1 = (bf16[128,7168]{1,0:T(8,128)(2,1)}, bf16[2,2304,512]{2,1,0:T(8,128)(2,1)}, bf16[2,64,2304]{2,1,0:T(8,128)(2,1)}) custom-call(s32[2]{0:T(128)} %len_ref.3, bf16[128,7168]{1,0:T(8,128)(2,1)} %get-tuple-element.9.y_hbm, bf16[2,2304,512]{2,1,0:T(8,128)(2,1)} %c_hbm.3, bf16[2,64,2304]{2,1,0:T(8,128)(2,1)} %bitcast.18, ...), custom_call_target="tpu_custom_call" | custom-call | flops 4000000000 | bytes 12582912 | tf_op jit(solution)/shard_map/caches/pallas_call | solution.py:109
